TPU v7x, 32 devices: a whole 2x2x4 slice. The times are simulated.
32 devices in a mesh: pipe: 4 (over y, core), vocab: 2 (over x), expert: 4 (over z).
Axes of the slice: x: 2, y: 2, z: 4, core: 2. Of those that a mesh axis runs over, the one named last changes fastest.
Arguments:
- token_ids: int32 [192], replicated, may hold values from 0 to 65535
- routes: int32 [192, 2], replicated, may hold values from 0 to 3, all different within a row; in each aligned block of 192 rows (0 to 191, 192 to 383, ...) at most 144 rows name the same one
- gate_weights: float32 [192, 2], replicated, may hold values from 0.2 to 1
- embed_table: bfloat16 [65536, 7168], P(('pipe', 'vocab'), 'expert'), may hold values from -0.59765625 to 0.59765625
- w_gate: bfloat16 [4, 7168, 2048], P('expert', None, ('pipe', 'vocab')), may hold values from -0.5 to 0.5
- w_up: bfloat16 [4, 7168, 2048], P('expert', None, ('pipe', 'vocab')), may hold values from -0.5 to 0.5
- w_down: bfloat16 [4, 2048, 7168], P('expert', ('pipe', 'vocab')), may hold values from -0.125 to 0.125
Outputs:
- logits: bfloat16 [192, 65536], P('expert', ('pipe', 'vocab'))
Inputs may be any that keep to these rules, and one draw needn't show every extreme that they name: `routes`: each row names 2 different experts; over all 192 rows no expert is named more than 144 times, a bound that some block reaches.
All inputs are finite; a program needn't handle non-finite values.
Results may differ from a plain program's by a relative error of at most 0.025.
Values may be sent and summed in bfloat16 or wider, within the bound.
A program may use at most 128 MiB of HBM per device.

v0:
```python
import jax
import jax.numpy as jnp
from jax import lax
from jax.sharding import PartitionSpec as P


def per_device(token_ids, routes, gate_weights, embed_table, w_gate, w_up, w_down):
    vocab_rows, width_cols = embed_table.shape
    tokens, top_count = routes.shape
    experts = lax.axis_size("expert")
    group_size = lax.axis_size(("pipe", "vocab"))
    capacity = group_size * (3 * tokens * top_count // (2 * experts * group_size))
    row_base = lax.axis_index(("pipe", "vocab")) * vocab_rows
    local_ids = token_ids - row_base
    in_shard = (local_ids >= 0) & (local_ids < vocab_rows)
    lookup_rows = jnp.take(embed_table, jnp.clip(local_ids, 0, vocab_rows - 1), axis=0)
    lookup_rows = jnp.where(in_shard[:, None], lookup_rows.astype(jnp.float32), 0.0)
    embedded = lax.psum(lookup_rows.astype(jnp.bfloat16), ("pipe", "vocab"))
    flat_routes = routes.reshape(-1)
    one_hot = (flat_routes[:, None] == jnp.arange(experts, dtype=jnp.int32)[None, :]).astype(
        jnp.int32
    )
    slot_index = jnp.sum((jnp.cumsum(one_hot, axis=0) - one_hot) * one_hot, axis=1)
    slot_dest = flat_routes * capacity + slot_index
    repeated = jnp.repeat(embedded, top_count, axis=0)
    buffer = jnp.zeros((experts * capacity, width_cols), jnp.bfloat16).at[slot_dest].set(repeated)
    buffer = buffer.reshape(experts, capacity, width_cols)
    flat_rows = lax.all_to_all(buffer, "expert", split_axis=0, concat_axis=2, tiled=True)[0]
    gate_proj = jnp.dot(flat_rows, w_gate[0], preferred_element_type=jnp.float32)
    up_proj = jnp.dot(flat_rows, w_up[0], preferred_element_type=jnp.float32)
    hidden = (jax.nn.silu(gate_proj) * up_proj).astype(jnp.bfloat16)
    partial_value = jnp.dot(hidden, w_down[0], preferred_element_type=jnp.float32)[None]
    shared = lax.psum_scatter(
        partial_value.astype(jnp.bfloat16), ("pipe", "vocab"), scatter_dimension=1, tiled=True
    ).astype(jnp.float32)
    shared = lax.all_to_all(
        shared.astype(jnp.bfloat16), "expert", split_axis=2, concat_axis=0, tiled=True
    ).astype(shared.dtype)
    returned = lax.all_gather(
        shared.astype(jnp.bfloat16), ("pipe", "vocab"), axis=1, tiled=True
    ).astype(shared.dtype)
    picked = returned.reshape(experts * capacity, width_cols)[slot_dest].reshape(
        tokens, top_count, width_cols
    )
    moe_out = jnp.sum(picked * gate_weights[:, :, None], axis=1)
    residual = (embedded.astype(jnp.float32) + moe_out).astype(jnp.bfloat16)
    return lax.psum_scatter(
        lax.dot_general(
            residual, embed_table, (((1,), (1,)), ((), ())), preferred_element_type=jnp.float32
        ).astype(jnp.bfloat16),
        "expert",
        scatter_dimension=0,
        tiled=True,
    )


def solution(mesh):
    return jax.shard_map(
        per_device,
        mesh=mesh,
        in_specs=(
            P(),
            P(),
            P(),
            P(("pipe", "vocab"), "expert"),
            P("expert", None, ("pipe", "vocab")),
            P("expert", None, ("pipe", "vocab")),
            P("expert", ("pipe", "vocab"), None),
        ),
        out_specs=P("expert", ("pipe", "vocab")),
        check_vma=False,
    )
```

profile of v0, /device:TPU:0, one launch (start us, length us, event | category | flops | bytes accessed | tf_op | source)
XLA Modules:
  0.0 428.2 jit_solution(8567750402209135640)
XLA Ops:
  6.5 0.0 all-reduce.4.cloned.1.call-start
  6.5 0.7 compare_and_fusion
  7.2 14.9 %gather_fusion = bf16[192,1792]{1,0:T(8,128)(2,1)S(1)} fusion(bf16[8192,1792]{1,0:T(8,128)(2,1)} %param.10, s32[1024]{0:T(1024)S(1)} %pad_clamp_fusion.1), kind=kCustom, calls=%fused_computation | custom fusion | bytes 1377024 | tf_op jit(solution)/shard_map/jit(_take)/gather | solution.py:16
  22.1 0.0 copy-start.2
  22.1 1.2 select_convert_fusion
  23.3 0.0 all-reduce.4.cloned.1.call-update
  23.3 0.0 all-gather.3.cloned.1.call-start
  23.4 0.0 copy-done.2
  23.4 0.1 copy.39
  23.5 0.1 eq.29
  23.7 0.1 eq.25
  23.8 1.2 reduce-window.6
  25.1 0.2 slice_reduce_fusion
  25.3 0.2 reduce-window.9
  25.5 0.1 copy.38
  25.6 0.1 mul.44
  25.7 0.1 add_bitcast_fusion
  25.9 55.8 %all-reduce.4.cloned.1.call-done = bf16[192,1792]{1,0:T(8,128)(2,1)} async-done(((bf16[192,1792]{1,0:T(8,128)(2,1)}), bf16[192,1792]{1,0:T(8,128)(2,1)}) %all-reduce.4.cloned.1.call-update) | async-done | bytes 688144 | tf_op jit(solution)/shard_map/psum | solution.py:18
  81.6 1.8 broadcast_in_dim.42
  83.4 0.6 reshape.98
  84.0 3.3 scatter_custom_fusion
  87.3 51.2 %all_to_all.33 = bf16[4,144,1792]{2,1,0:T(8,128)(2,1)S(1)} all-to-all(bf16[4,144,1792]{2,1,0:T(8,128)(2,1)S(1)} %bitcast.66), channel_id=1, replica_groups=mesh['pipe'=4,'vocab'=2,'expert'=4] {'expert'}, dimensions={0} | all-to-all | bytes 4128768 | tf_op jit(solution)/shard_map/all_to_all | solution.py:28
  138.5 1.1 copy.41
  139.5 0.0 copy-start
  139.6 0.3 copy.50
  139.8 1.8 copy-done
  141.6 0.8 fusion.5
  142.4 6.9 %fusion.1 = bf16[1,144,7168]{2,1,0:T(8,128)(2,1)} fusion(bf16[1,256,7168]{2,1,0:T(8,128)(2,1)} %param.13, bf16[144,7168]{1,0:T(8,128)(2,1)S(1)} %bitcast.63, bf16[1,7168,256]{2,1,0:T(8,128)(2,1)} %param.12, f32[144,256]{1,0:T(8,128)S(1)} %fusion.5), kind=kOutput, calls=%fused_computation.5 | convolution fusion | flops 1058217984 | bytes 11616256 | tf_op jit(solution)/shard_map/dot_general | solution.py:32
  149.2 0.0 copy-start.4
  149.2 58.3 %fusion = bf16[24,7168]{1,0:T(8,128)(2,1)S(1)} fusion(bf16[1,144,7168]{2,1,0:T(8,128)(2,1)} %fusion.1), kind=kCustom, calls=%all-reduce-scatter | all-reduce-scatter fusion | flops 1376257 | bytes 2408960
  207.6 1.9 collective-permute-start
  209.5 0.1 slice.13
  209.6 1.7 collective-permute-start.1
  211.3 0.0 copy-done.4
  211.3 0.6 dynamic-slice.4
  212.6 0.0 collective-permute-done.1
  212.6 4.5 %collective-permute-done = bf16[24,7168]{1,0:T(8,128)(2,1)S(1)} collective-permute-done((bf16[24,7168]{1,0:T(8,128)(2,1)S(1)}, bf16[24,7168]{1,0:T(8,128)(2,1)S(1)}, u32[]{:S(2)}, u32[]{:S(2)}) %collective-permute-start) | collective-permute-done | bytes 344096
  217.0 4.8 %concatenate = bf16[66,7168]{1,0:T(8,128)(2,1)S(1)} concatenate(bf16[18,7168]{1,0:T(8,128)(2,1)S(1)} %collective-permute-done.1, bf16[24,7168]{1,0:T(8,128)(2,1)S(1)} %collective-permute-done, bf16[24,7168]{1,0:T(8,128)(2,1)S(1)} %fusion), dimensions={0} | concatenate | bytes 1892352
  221.9 0.1 dynamic-slice_bitcast_fusion
  222.0 6.0 %copy.42 = bf16[1,18,7168]{1,0,2:T(2,128)(2,1)} copy(bf16[1,18,7168]{2,1,0:T(8,128)(2,1)S(1)} %dynamic-slice_bitcast_fusion) | data formatting | bytes 516096 | tf_op jit(solution)/shard_map/reduce_scatter | solution.py:33
  228.0 0.5 broadcast.68
  228.5 39.8 %reduce.4 = bf16[7168,18]{1,0:T(8,128)(2,1)S(1)} reduce(bf16[7168,1,18]{2,1,0:T(2,128)(2,1)} %bitcast.64, bf16[]{:T(256)} %broadcast.68), dimensions={1}, to_apply=%bitcast.56.reduce_sub_computation | reduce | bytes 516098
  268.3 3.4 reshape.114
  271.7 9.8 %all_to_all.34 = bf16[4,2,16128]{2,1,0:T(2,128)(2,1)S(1)} all-to-all(bf16[4,2,16128]{2,1,0:T(2,128)(2,1)S(1)} %reshape.114), channel_id=1, replica_groups=mesh['pipe'=4,'vocab'=2,'expert'=4] {'expert'}, dimensions={0} | all-to-all | bytes 516096 | tf_op jit(solution)/shard_map/all_to_all | solution.py:36
  281.4 5.2 %reshape.115 = bf16[7168,1,18]{2,1,0:T(2,128)(2,1)} reshape(bf16[4,2,16128]{2,1,0:T(2,128)(2,1)S(1)} %all_to_all.34) | data formatting | bytes 516096
  286.6 0.0 copy-start.3
  286.6 7.3 %copy.43 = bf16[1,18,7168]{2,1,0:T(8,128)(2,1)S(1)} copy(bf16[1,18,7168]{1,0,2:T(2,128)(2,1)} %bitcast.65) | data formatting | bytes 516096 | tf_op jit(solution)/shard_map/all_to_all | solution.py:36
  293.9 0.8 all_to_all.28
  294.7 0.0 all-gather.3.cloned.1.call-update
  294.7 0.3 reduce-scatter.5.cloned.1.call-start
  295.0 0.0 copy-done.3
  295.0 0.1 copy.46
  295.1 29.7 %all-gather.3.cloned.1.call-done = bf16[4,1,144,1792]{3,0,1,2:T(4,128)(2,1)} async-done(((bf16[4,1,18,1792]{3,0,1,2:T(4,128)(2,1)}), bf16[4,1,144,1792]{3,0,1,2:T(4,128)(2,1)}) %all-gather.3.cloned.1.call-update) | async-done | bytes 2064400 | tf_op jit(solution)/shard_map/all_gather | solution.py:39
  324.8 1.8 copy.45
  326.6 2.4 bitcast_convert_fusion
  329.0 6.1 %gather_fusion.1 = f32[384,1792]{1,0:T(8,128)S(1)} fusion(f32[576,1792]{1,0:T(8,128)} %bitcast_convert_fusion, s32[1024]{0:T(1024)S(1)} %pad_clamp_fusion), kind=kCustom, calls=%fused_computation.1 | custom fusion | bytes 5506560 | tf_op jit(solution)/shard_map/gather | solution.py:42
  335.1 2.8 reshape.75
  337.8 0.0 copy-start.1
  337.8 5.9 %multiply_reduce_fusion = f32[192,1792]{1,0:T(8,128)S(1)} fusion(f32[192,2,1792]{2,1,0:T(2,128)} %reshape.75, f32[192,2]{1,0:T(8,128)S(1)} %copy.46), kind=kLoop, calls=%fused_computation.11 | loop fusion | flops 1032192 | bytes 4130304 | tf_op jit(solution)/shard_map/reduce_sum | solution.py:45
  343.7 0.0 copy-done.1
  343.8 17.4 %convolution_convert_fusion = bf16[192,8192]{1,0:T(8,128)(2,1)} fusion(bf16[8192,1792]{1,0:T(8,128)(2,1)} %param.10, f32[192,1792]{1,0:T(8,128)S(1)} %multiply_reduce_fusion, bf16[192,1792]{1,0:T(8,128)(2,1)S(1)} %copy-done.1), kind=kOutput, calls=%fused_computation.3 | convolution fusion | flops 5639749632 | bytes 34570240 | tf_op jit(solution)/shard_map/dot_general | solution.py:48
  361.1 0.0 reduce-scatter.5.cloned.1.call-update
  361.1 60.6 %reduce-scatter.5.cloned.1.call-done = bf16[48,8192]{1,0:T(8,128)(2,1)} async-done(((bf16[192,8192]{1,0:T(8,128)(2,1)}), bf16[48,8192]{1,0:T(8,128)(2,1)}) %reduce-scatter.5.cloned.1.call-update) | async-done | bytes 786448 | tf_op jit(solution)/shard_map/reduce_scatter | solution.py:47
  (6 shorter events, 0.1 us)
Async XLA Ops:
  6.5 75.1 %all-reduce.4.cloned.1.call-start = ((), (), s32[]{:S(2)}) async-start(), calls=%async_computation.3 | async-start | bytes 1376256 | tf_op jit(solution)/shard_map/psum | solution.py:18
  22.1 1.3 copy-start.2
  23.3 301.5 %all-gather.3.cloned.1.call-start = ((), (), s32[]{:S(2)}) async-start(), calls=%async_computation.5 | async-start | bytes 2322432 | tf_op jit(solution)/shard_map/all_gather | solution.py:39
  139.5 2.0 copy-start
  149.2 62.1 %copy-start.4 = (u32[32]{0:T(128)S(1)}, u32[32]{0:T(128)}, u32[]{:S(2)}) copy-start(u32[32]{0:T(128)} %constant.54) | copy-start | bytes 388
  207.6 9.5 %collective-permute-start = (bf16[24,7168]{1,0:T(8,128)(2,1)S(1)}, bf16[24,7168]{1,0:T(8,128)(2,1)S(1)}, u32[]{:S(2)}, u32[]{:S(2)}) collective-permute-start(bf16[24,7168]{1,0:T(8,128)(2,1)S(1)} %fusion), channel_id=1, source_target_pairs={{0,4},{4,8},{8,12},{12,16},{16,20},{20,24},{24,28},{1,5},{5,9},{9,... | collective-permute-start | bytes 1032200
  209.6 3.0 collective-permute-start.1
  286.6 8.4 %copy-start.3 = (f32[192,2]{0,1:T(2,128)S(1)}, f32[192,2]{0,1:T(2,128)}, u32[]{:S(2)}) copy-start(f32[192,2]{0,1:T(2,128)} %param.9) | copy-start | bytes 4612
  294.7 127.0 %reduce-scatter.5.cloned.1.call-start = ((), (), s32[]{:S(2)}) async-start(), calls=%async_computation.4 | async-start | bytes 3932160 | tf_op jit(solution)/shard_map/reduce_scatter | solution.py:47
  337.8 5.9 %copy-start.1 = (bf16[192,1792]{1,0:T(8,128)(2,1)S(1)}, bf16[192,1792]{1,0:T(8,128)(2,1)}, u32[]{:S(2)}) copy-start(bf16[192,1792]{1,0:T(8,128)(2,1)} %all-reduce.4.cloned.1.call-done) | copy-start | bytes 2064388
Sparse Core Ops, SparseCore 0:
  23.5 58.1 all-reduce.3
  294.8 29.9 all-gather.2
  361.3 60.3 reduce-scatter.4
where the time goes:
time: 429 us; the launch traced here: 428 us
  waiting for transfers between devices  151 us (35%)
  blocking collectives  119 us (28%)
  local copies, waits for them, and re-layouts  64 us (15%)
  other arithmetic  51.5 us (12%)
  matrix products  25 us (6%)
  between operations  14 us (3%)
    reduce_scatter x1, waiting for transfers between devices, per_device(): lax.psum_scatter(lax.dot_general(residual, embed_table, (((1,), (1,)), ((...  60.6 us
    unnamed x1, blocking collectives  58.3 us
    psum x1, waiting for transfers between devices, per_device(): embedded = lax.psum(lookup_rows.astype(jnp.bfloat16), ('pipe', 'vocab'))  55.8 us
    all_to_all x1, blocking collectives, per_device(): lax.all_to_all(buffer, 'expert', split_axis=0, concat_axis=2, tiled=True)[0]  51.2 us
    unnamed x2, other arithmetic  39.8 us
    all_gather x1, waiting for transfers between devices, per_device(): lax.all_gather(shared.astype(jnp.bfloat16), ('pipe', 'vocab'), axis=1, ti...  29.7 us
    dot_general x1, matrix products, per_device(): lax.dot_general(residual, embed_table, (((1,), (1,)), ((), ())), preferre...  17.4 us
    unnamed x20, local copies, waits for them, and re-layouts  16.9 us
  transfers between devices with their start and end apart: 5, of which 4 were waited for; matrix products, arithmetic and copies ran while one was open for 1% of the time, Pallas kernels for 0%

commit v1 on v0

--- a/solution.py
+++ b/solution.py
@@ -2,6 +2,13 @@
 import jax.numpy as jnp
 from jax import lax
 from jax.sharding import PartitionSpec as P
+
+
+def all_by_exchange(x, axis, d):
+    peers = lax.axis_size(axis)
+    blocks = jnp.stack([x for _ in range(peers)])
+    blocks = lax.all_to_all(blocks, axis, split_axis=0, concat_axis=0)
+    return jnp.concatenate(blocks, axis=d)
 
 
 def per_device(token_ids, routes, gate_weights, embed_table, w_gate, w_up, w_down):
@@ -36,9 +43,9 @@
     shared = lax.all_to_all(
         shared.astype(jnp.bfloat16), "expert", split_axis=2, concat_axis=0, tiled=True
     ).astype(shared.dtype)
-    returned = lax.all_gather(
-        shared.astype(jnp.bfloat16), ("pipe", "vocab"), axis=1, tiled=True
-    ).astype(shared.dtype)
+    returned = all_by_exchange(shared.astype(jnp.bfloat16), ("pipe", "vocab"), 1).astype(
+        shared.dtype
+    )
     picked = returned.reshape(experts * capacity, width_cols)[slot_dest].reshape(
         tokens, top_count, width_cols
     )

time: 429 us -> 454 us (1.058); the launches traced: 428 us -> 446 us
  blocking collectives: 119 us -> 130 us
  local copies, waits for them, and re-layouts: 64 us -> 71.9 us
  waiting for transfers between devices: 151 us -> 144 us
  starting transfers between devices: 3.96 us -> 10.7 us
    all_gather x1 -> x0, waiting for transfers between devices: 29.7 us -> none  [per_device(): lax.all_gather(shared.astype(jnp.bfloat16), ('pipe', 'vocab'), axis=1, ti...]
    all_to_all x0 -> x1, waiting for transfers between devices: none -> 25.3 us  [all_by_exchange(): blocks = lax.all_to_all(blocks, axis, split_axis=0, concat_axis=0)]
    all_to_all x1, blocking collectives: 51.2 us -> 61.5 us  [per_device(): lax.all_to_all(buffer, 'expert', split_axis=0, concat_axis=2, tiled=True)[0]]
    convert_element_type x0 -> x2, local copies, waits for them, and re-layouts: none -> 8.49 us  [per_device(): all_by_exchange(shared.astype(jnp.bfloat16), ('pipe', 'vocab'), 1)]
    all_to_all x0 -> x1, starting transfers between devices: none -> 6.8 us  [all_by_exchange(): blocks = lax.all_to_all(blocks, axis, split_axis=0, concat_axis=0)]
where the time goes in v1:
time: 454 us; the launch traced here: 446 us
  waiting for transfers between devices  144 us (32%)
  blocking collectives  130 us (29%)
  local copies, waits for them, and re-layouts  71.9 us (16%)
  other arithmetic  49.6 us (11%)
  matrix products  25 us (6%)
  between operations  14.7 us (3%)
  starting transfers between devices  10.7 us (2%)
    all_to_all x1, blocking collectives, per_device(): lax.all_to_all(buffer, 'expert', split_axis=0, concat_axis=2, tiled=True)[0]  61.5 us
    reduce_scatter x1, waiting for transfers between devices, per_device(): lax.psum_scatter(lax.dot_general(residual, embed_table, (((1,), (1,)), ((...  58.5 us
    unnamed x1, blocking collectives  58.3 us
    psum x1, waiting for transfers between devices, per_device(): embedded = lax.psum(lookup_rows.astype(jnp.bfloat16), ('pipe', 'vocab'))  55.8 us
    unnamed x2, other arithmetic  39.8 us
    all_to_all x1, waiting for transfers between devices, all_by_exchange(): blocks = lax.all_to_all(blocks, axis, split_axis=0, concat_axis=0)  25.3 us
    dot_general x1, matrix products, per_device(): lax.dot_general(residual, embed_table, (((1,), (1,)), ((), ())), preferre...  17.3 us
    unnamed x20, local copies, waits for them, and re-layouts  16.9 us
  transfers between devices with their start and end apart: 5, of which 4 were waited for; matrix products, arithmetic and copies ran while one was open for 1% of the time, Pallas kernels for 0%

profile of v1, /device:TPU:0, one launch (start us, length us, event | category | flops | bytes accessed | tf_op | source)
XLA Modules:
  0.0 445.6 jit_solution(3523570906340268795)
XLA Ops:
  6.5 0.0 all-reduce.4.cloned.1.call-start
  6.5 0.7 compare_and_fusion
  7.2 0.0 copy-start.2
  7.2 14.9 %gather_fusion = bf16[192,1792]{1,0:T(8,128)(2,1)S(1)} fusion(bf16[8192,1792]{1,0:T(8,128)(2,1)} %param.10, s32[1024]{0:T(1024)S(1)} %pad_clamp_fusion.1), kind=kCustom, calls=%fused_computation | custom fusion | bytes 1377024 | tf_op jit(solution)/shard_map/jit(_take)/gather | solution.py:23
  22.1 1.2 select_convert_fusion
  23.3 0.0 all-reduce.4.cloned.1.call-update
  23.4 0.0 copy-done.2
  23.4 0.1 copy.30
  23.5 0.1 eq.29
  23.6 0.1 eq.25
  23.8 1.2 reduce-window.6
  25.0 0.2 slice_reduce_fusion
  25.2 0.2 reduce-window.9
  25.4 0.1 copy.29
  25.6 0.1 mul.44
  25.7 0.1 add_bitcast_fusion
  25.8 55.8 %all-reduce.4.cloned.1.call-done = bf16[192,1792]{1,0:T(8,128)(2,1)} async-done(((bf16[192,1792]{1,0:T(8,128)(2,1)}), bf16[192,1792]{1,0:T(8,128)(2,1)}) %all-reduce.4.cloned.1.call-update) | async-done | bytes 688144 | tf_op jit(solution)/shard_map/psum | solution.py:25
  81.6 1.8 broadcast_in_dim.42
  83.5 0.6 reshape.98
  84.0 3.3 scatter_custom_fusion
  87.3 61.5 %all_to_all.35 = bf16[4,144,1792]{2,1,0:T(8,128)(2,1)S(1)} all-to-all(bf16[4,144,1792]{2,1,0:T(8,128)(2,1)S(1)} %bitcast.65), channel_id=1, replica_groups=mesh['pipe'=4,'vocab'=2,'expert'=4] {'expert'}, dimensions={0} | all-to-all | bytes 4128768 | tf_op jit(solution)/shard_map/all_to_all | solution.py:35
  148.9 1.1 copy.32
  149.9 0.0 copy-start
  149.9 0.3 copy.40
  150.2 1.8 copy-done
  152.0 0.8 fusion.5
  152.8 6.9 %fusion.1 = bf16[1,144,7168]{2,1,0:T(8,128)(2,1)} fusion(bf16[1,256,7168]{2,1,0:T(8,128)(2,1)} %param.13, bf16[144,7168]{1,0:T(8,128)(2,1)S(1)} %bitcast.62, bf16[1,7168,256]{2,1,0:T(8,128)(2,1)} %param.12, f32[144,256]{1,0:T(8,128)S(1)} %fusion.5), kind=kOutput, calls=%fused_computation.5 | convolution fusion | flops 1058217984 | bytes 11616256 | tf_op jit(solution)/shard_map/dot_general | solution.py:39
  159.6 0.0 copy-start.4
  159.6 58.3 %fusion = bf16[24,7168]{1,0:T(8,128)(2,1)S(1)} fusion(bf16[1,144,7168]{2,1,0:T(8,128)(2,1)} %fusion.1), kind=kCustom, calls=%all-reduce-scatter | all-reduce-scatter fusion | flops 1376257 | bytes 2408960
  217.9 2.0 collective-permute-start
  219.9 0.1 slice.13
  220.0 1.7 collective-permute-start.1
  221.7 0.0 copy-done.4
  221.7 0.6 dynamic-slice.4
  222.9 0.0 collective-permute-done.1
  222.9 4.5 %collective-permute-done = bf16[24,7168]{1,0:T(8,128)(2,1)S(1)} collective-permute-done((bf16[24,7168]{1,0:T(8,128)(2,1)S(1)}, bf16[24,7168]{1,0:T(8,128)(2,1)S(1)}, u32[]{:S(2)}, u32[]{:S(2)}) %collective-permute-start) | collective-permute-done | bytes 344096
  227.4 4.8 %concatenate = bf16[66,7168]{1,0:T(8,128)(2,1)S(1)} concatenate(bf16[18,7168]{1,0:T(8,128)(2,1)S(1)} %collective-permute-done.1, bf16[24,7168]{1,0:T(8,128)(2,1)S(1)} %collective-permute-done, bf16[24,7168]{1,0:T(8,128)(2,1)S(1)} %fusion), dimensions={0} | concatenate | bytes 1892352
  232.2 0.1 dynamic-slice_bitcast_fusion
  232.3 6.0 %copy.33 = bf16[1,18,7168]{1,0,2:T(2,128)(2,1)} copy(bf16[1,18,7168]{2,1,0:T(8,128)(2,1)S(1)} %dynamic-slice_bitcast_fusion) | data formatting | bytes 516096 | tf_op jit(solution)/shard_map/reduce_scatter | solution.py:40
  238.4 0.5 broadcast.69
  238.9 39.8 %reduce.4 = bf16[7168,18]{1,0:T(8,128)(2,1)S(1)} reduce(bf16[7168,1,18]{2,1,0:T(2,128)(2,1)} %bitcast.63, bf16[]{:T(256)} %broadcast.69), dimensions={1}, to_apply=%bitcast.55.reduce_sub_computation | reduce | bytes 516098
  278.7 3.4 reshape.110
  282.1 9.7 %all_to_all.36 = bf16[4,2,16128]{2,1,0:T(2,128)(2,1)S(1)} all-to-all(bf16[4,2,16128]{2,1,0:T(2,128)(2,1)S(1)} %reshape.110), channel_id=1, replica_groups=mesh['pipe'=4,'vocab'=2,'expert'=4] {'expert'}, dimensions={0} | all-to-all | bytes 516096 | tf_op jit(solution)/shard_map/all_to_all | solution.py:43
  291.8 5.2 %reshape.111 = bf16[7168,1,18]{2,1,0:T(2,128)(2,1)} reshape(bf16[4,2,16128]{2,1,0:T(2,128)(2,1)S(1)} %all_to_all.36) | data formatting | bytes 516096
  297.0 7.3 %copy.34 = bf16[1,18,7168]{2,1,0:T(8,128)(2,1)S(1)} copy(bf16[1,18,7168]{1,0,2:T(2,128)(2,1)} %bitcast.64) | data formatting | bytes 516096 | tf_op jit(solution)/shard_map/all_to_all | solution.py:43
  304.2 0.1 all_to_all.29
  304.4 0.0 copy-start.3
  304.4 1.9 stack.5
  306.2 6.8 %all-to-all-start.2 = ((bf16[8,4,18,1792]{3,1,2,0:T(4,128)(2,1)}), bf16[8,4,18,1792]{3,1,2,0:T(4,128)(2,1)S(1)}, u32[]{:S(2)}, u32[]{:S(2)}) async-start(bf16[8,4,18,1792]{3,1,2,0:T(4,128)(2,1)} %stack.5), calls=%async_computation.2 | async-start | bytes 4128768 | tf_op jit(solution)/shard_map/all_to_all | solution.py:10
  313.0 0.2 reduce-scatter.5.cloned.1.call-start
  313.3 0.0 copy-done.3
  313.3 0.1 copy.36
  313.4 25.3 %all-to-all-done.2 = bf16[8,4,18,1792]{3,1,2,0:T(4,128)(2,1)S(1)} async-done(((bf16[8,4,18,1792]{3,1,2,0:T(4,128)(2,1)}), bf16[8,4,18,1792]{3,1,2,0:T(4,128)(2,1)S(1)}, u32[]{:S(2)}, u32[]{:S(2)}) %all-to-all-start.2) | async-done | bytes 2064416 | tf_op jit(solution)/shard_map/all_to_all | solution.py:10
  338.7 0.5 convert_bitcast_fusion
  339.3 3.3 copy.35
  342.5 5.2 %reshape.77 = f32[576,1792]{1,0:T(8,128)} reshape(f32[4,8,18,1792]{3,2,1,0:T(8,128)} %copy.35) | data formatting | bytes 8257536 | tf_op jit(solution)/shard_map/convert_element_type | solution.py:46
  347.8 6.1 %gather_fusion.1 = f32[384,1792]{1,0:T(8,128)S(1)} fusion(f32[576,1792]{1,0:T(8,128)} %reshape.77, s32[1024]{0:T(1024)S(1)} %pad_clamp_fusion), kind=kCustom, calls=%fused_computation.1 | custom fusion | bytes 5506560 | tf_op jit(solution)/shard_map/gather | solution.py:49
  353.8 2.8 reshape.76
  356.6 0.0 copy-start.1
  356.6 5.9 %multiply_reduce_fusion = f32[192,1792]{1,0:T(8,128)S(1)} fusion(f32[192,2,1792]{2,1,0:T(2,128)} %reshape.76, f32[192,2]{1,0:T(8,128)S(1)} %copy.36), kind=kLoop, calls=%fused_computation.12 | loop fusion | flops 1032192 | bytes 4130304 | tf_op jit(solution)/shard_map/reduce_sum | solution.py:52
  362.5 0.0 copy-done.1
  362.5 17.3 %convolution_convert_fusion = bf16[192,8192]{1,0:T(8,128)(2,1)} fusion(bf16[8192,1792]{1,0:T(8,128)(2,1)} %param.10, f32[192,1792]{1,0:T(8,128)S(1)} %multiply_reduce_fusion, bf16[192,1792]{1,0:T(8,128)(2,1)S(1)} %copy-done.1), kind=kOutput, calls=%fused_computation.3 | convolution fusion | flops 5639749632 | bytes 34570240 | tf_op jit(solution)/shard_map/dot_general | solution.py:55
  379.9 0.0 reduce-scatter.5.cloned.1.call-update
  379.9 58.5 %reduce-scatter.5.cloned.1.call-done = bf16[48,8192]{1,0:T(8,128)(2,1)} async-done(((bf16[192,8192]{1,0:T(8,128)(2,1)}), bf16[48,8192]{1,0:T(8,128)(2,1)}) %reduce-scatter.5.cloned.1.call-update) | async-done | bytes 786448 | tf_op jit(solution)/shard_map/reduce_scatter | solution.py:54
  (6 shorter events, 0.1 us)
Async XLA Ops:
  6.5 75.1 %all-reduce.4.cloned.1.call-start = ((), (), s32[]{:S(2)}) async-start(), calls=%async_computation.4 | async-start | bytes 1376256 | tf_op jit(solution)/shard_map/psum | solution.py:25
  7.2 16.1 %copy-start.2 = (s32[192,2]{0,1:T(2,128)S(1)}, s32[192,2]{0,1:T(2,128)}, u32[]{:S(2)}) copy-start(s32[192,2]{0,1:T(2,128)} %param.8) | copy-start | bytes 4612
  149.9 2.0 copy-start
  159.6 62.1 %copy-start.4 = (u32[32]{0:T(128)S(1)}, u32[32]{0:T(128)}, u32[]{:S(2)}) copy-start(u32[32]{0:T(128)} %constant.54) | copy-start | bytes 388
  217.9 9.5 %collective-permute-start = (bf16[24,7168]{1,0:T(8,128)(2,1)S(1)}, bf16[24,7168]{1,0:T(8,128)(2,1)S(1)}, u32[]{:S(2)}, u32[]{:S(2)}) collective-permute-start(bf16[24,7168]{1,0:T(8,128)(2,1)S(1)} %fusion), channel_id=1, source_target_pairs={{0,4},{4,8},{8,12},{12,16},{16,20},{20,24},{24,28},{1,5},{5,9},{9,... | collective-permute-start | bytes 1032200
  220.0 3.0 collective-permute-start.1
  304.4 8.9 %copy-start.3 = (f32[192,2]{0,1:T(2,128)S(1)}, f32[192,2]{0,1:T(2,128)}, u32[]{:S(2)}) copy-start(f32[192,2]{0,1:T(2,128)} %param.9) | copy-start | bytes 4612
  306.2 32.5 %all-to-all-start.2 = ((bf16[8,4,18,1792]{3,1,2,0:T(4,128)(2,1)}), bf16[8,4,18,1792]{3,1,2,0:T(4,128)(2,1)S(1)}, u32[]{:S(2)}, u32[]{:S(2)}) async-start(bf16[8,4,18,1792]{3,1,2,0:T(4,128)(2,1)} %stack.5), calls=%async_computation.2 | async-start | bytes 4128768 | tf_op jit(solution)/shard_map/all_to_all | solution.py:10
  313.0 125.3 %reduce-scatter.5.cloned.1.call-start = ((), (), s32[]{:S(2)}) async-start(), calls=%async_computation.5 | async-start | bytes 3932160 | tf_op jit(solution)/shard_map/reduce_scatter | solution.py:54
  356.6 5.9 %copy-start.1 = (bf16[192,1792]{1,0:T(8,128)(2,1)S(1)}, bf16[192,1792]{1,0:T(8,128)(2,1)}, u32[]{:S(2)}) copy-start(bf16[192,1792]{1,0:T(8,128)(2,1)} %all-reduce.4.cloned.1.call-done) | copy-start | bytes 2064388
Sparse Core Ops, SparseCore 0:
  23.5 58.1 all-reduce.3
  380.0 58.3 reduce-scatter.4
